TPU v7x, 32 devices: a whole 2x2x4 slice. The times are simulated.
32 devices in a mesh: section: 4 (over z), ctx: 4 (over x, core), tp: 2 (over y).
Axes of the slice: x: 2, y: 2, z: 4, core: 2. Of those that a mesh axis runs over, the one named last changes fastest.
Arguments:
- queries: bfloat16 [4, 512, 8192], P('section', 'ctx', 'tp'), may hold values from -80 to 80
- keys: bfloat16 [4, 512, 1024], P('section', 'ctx', 'tp'), may hold values from -4 to 4
- values: bfloat16 [4, 512, 1024], P('section', 'ctx', 'tp'), may hold values from -6 to 6
- span_order: int32 [8], replicated, may hold values from 0 to 7, as said below
Outputs:
- attended: bfloat16 [4, 512, 8192], P('section', ('ctx', 'tp'))
Inputs may be any that keep to these rules, and one draw needn't show every extreme that they name: `span_order`: a permutation of 0 to 7 in which entries 2 c and 2 c + 1 sum to 7 for every c.
All inputs are finite; a program needn't handle non-finite values.
Results may differ from a plain program's by a relative error of at most 0.0055.
Values may be sent and summed in bfloat16 or wider, within the bound.
A program may use at most 64 MiB of HBM per device.

v0:
```python
import functools
import math

import jax
import jax.numpy as jnp
from jax import lax
from jax.experimental import pallas as pl
from jax.experimental.pallas import tpu as pltpu
from jax.sharding import PartitionSpec as P

HEAD = 128
MESH = pl.DeviceIdType.MESH
NEG = -1e30


def lanes(start, size):
    return pl.ds(pl.multiple_of(start, HEAD), size)


def kernel(
    n_sec, n_ctx, n_tp, heads_per_chunk,
    q_hbm, k_hbm, v_hbm, order_hbm, out_hbm,
    q_buf, q_in, k_own, v_own, k_all, v_all, o_buf, bias, order,
    q_sem, own_sem, order_sem, kv_send, kv_recv, z_send, z_recv, o_send, o_recv,
):
    sec, ctx, tp = lax.axis_index("section"), lax.axis_index("ctx"), lax.axis_index("tp")
    rows, q_cols = q_hbm.shape[1], q_hbm.shape[2]
    kv_heads = k_hbm.shape[2] // HEAD
    group = q_cols // k_hbm.shape[2]
    g = heads_per_chunk
    chunk_cols = g * HEAD
    chunks = q_cols // chunk_cols
    per_kv = group // g
    out_rows = rows // n_tp
    keys = rows * n_ctx
    span = rows // 2
    local = kv_heads - 1
    group_cols = group * HEAD
    moved_cols = pl.ds(local * group_cols, group_cols)
    nxt, prv = lax.rem(sec + 1, n_sec), lax.rem(sec + n_sec - 1, n_sec)

    barrier = pltpu.get_barrier_semaphore()
    for t in range(n_tp):
        pl.semaphore_signal(barrier, inc=1, device_id=(prv, ctx, t), device_id_type=MESH)
    for d in range(1, n_ctx):
        pl.semaphore_signal(
            barrier, inc=1, device_id=(sec, lax.rem(ctx + d, n_ctx), tp), device_id_type=MESH
        )
    for d in range(1, n_tp):
        pl.semaphore_signal(
            barrier, inc=1, device_id=(sec, ctx, lax.rem(tp + d, n_tp)), device_id_type=MESH
        )
    own = []
    for i, (src, dst) in enumerate(((k_hbm, k_own), (v_hbm, v_own))):
        copy = pltpu.make_async_copy(src.at[0], dst, own_sem.at[i])
        copy.start()
        own.append(copy)
    order_copy = pltpu.make_async_copy(order_hbm, order, order_sem)
    order_copy.start()
    q_copies = []
    for i, h in enumerate([local, *range(local)]):
        cols = pl.ds(h * group_cols, group_cols)
        copy = pltpu.make_async_copy(q_hbm.at[0, :, cols], q_buf.at[:, cols], q_sem.at[i])
        copy.start()
        q_copies.append(copy)

    own[0].wait()
    own[1].wait()
    pl.semaphore_wait(barrier, n_ctx - 1 + n_tp + n_tp - 1)
    mine = pl.ds(pl.multiple_of(ctx * rows, rows), rows)

    def kv_copy(i, h, d):
        src, dst = ((k_own, k_all), (v_own, v_all))[i]
        peer = lax.rem(ctx + d, n_ctx)
        return pltpu.make_async_remote_copy(
            src_ref=src.at[:, pl.ds(h * HEAD, HEAD)] if h < local else dst.at[h, mine, :],
            dst_ref=dst.at[h, mine, :],
            send_sem=kv_send.at[h, i, d],
            recv_sem=kv_recv.at[h, i, d],
            device_id=(sec, peer, tp),
            device_id_type=MESH,
        )

    def kv_arrived(i, h, d):
        dst = (k_all, v_all)[i]
        peer = lax.rem(ctx + n_ctx - d, n_ctx)
        here = dst.at[h, pl.ds(pl.multiple_of(peer * rows, rows), rows), :]
        return pltpu.make_async_remote_copy(
            src_ref=here,
            dst_ref=here,
            send_sem=kv_send.at[h, i, d],
            recv_sem=kv_recv.at[h, i, d],
            device_id=(sec, lax.rem(ctx + d, n_ctx), tp),
            device_id_type=MESH,
        )

    def section_copy(i):
        if i < 2:
            src, dst = ((k_own, k_all), (v_own, v_all))[i]
            src, dst = src.at[:, pl.ds(local * HEAD, HEAD)], dst.at[local, mine, :]
        else:
            src, dst = q_buf.at[:, moved_cols], q_in
        return pltpu.make_async_remote_copy(
            src_ref=src,
            dst_ref=dst,
            send_sem=z_send.at[i],
            recv_sem=z_recv.at[i],
            device_id=(nxt, ctx, tp),
            device_id_type=MESH,
        )

    for h in range(local):
        for i in range(2):
            for d in range(1, n_ctx):
                kv_copy(i, h, d).start()
        if h == 0:
            section_copy(0).start()
            section_copy(1).start()
            q_copies[0].wait()
            section_copy(2).start()
    for h in range(local):
        k_all[h, mine, :] = k_own[:, h * HEAD : (h + 1) * HEAD]
        v_all[h, mine, :] = v_own[:, h * HEAD : (h + 1) * HEAD]

    order_copy.wait()
    row = lax.broadcasted_iota(jnp.int32, (rows, 1), 0)
    row_pos = jnp.where(row < span, order[2 * ctx] * span, order[2 * ctx + 1] * span - span) + row
    lane = lax.broadcasted_iota(jnp.int32, (1, keys), 1)
    key_pos = lane
    for j in range(keys // span):
        key_pos = jnp.where(
            (lane >= j * span) & (lane < (j + 1) * span), lane + (order[j] - j) * span, key_pos
        )
    bias[...] = jnp.where(key_pos <= row_pos, jnp.float32(0.0), jnp.float32(NEG))

    scale = math.log2(math.e) / math.sqrt(HEAD)

    def out_copy(c, t):
        return pltpu.make_async_remote_copy(
            src_ref=o_buf.at[c, pl.ds(pl.multiple_of(t * out_rows, out_rows), out_rows), :],
            dst_ref=out_hbm.at[0, :, lanes(tp * q_cols + c * chunk_cols, chunk_cols)],
            send_sem=o_send.at[c, t],
            recv_sem=o_recv.at[c, tp],
            device_id=(nxt, ctx, t),
            device_id_type=MESH,
        )

    def moved_out(c, d):
        t = lax.rem(tp + d, n_tp)
        src = o_buf.at[c, pl.ds(pl.multiple_of(t * out_rows, out_rows), out_rows), :]
        dst = out_hbm.at[0, :, lanes(tp * q_cols + c * chunk_cols, chunk_cols)]
        if d == 0:
            return pltpu.make_async_copy(src, dst, o_send.at[c, 0])
        return pltpu.make_async_remote_copy(
            src_ref=src,
            dst_ref=dst,
            send_sem=o_send.at[c, d],
            recv_sem=o_recv.at[c, tp],
            device_id=(sec, ctx, t),
            device_id_type=MESH,
        )

    for h in range(kv_heads):
        if h < local:
            q_copies[h + 1].wait()
        for d in range(1, n_ctx):
            kv_arrived(0, h, d).wait_recv()
        for d in range(1, n_ctx):
            kv_arrived(1, h, d).wait_recv()

        def chunk(i, _, h=h):
            c = h * per_kv + i
            q_ref, first = (q_buf, c * g) if h < local else (q_in, i * g)
            q = jnp.concatenate(
                [q_ref[:, lanes((first + j) * HEAD, HEAD)] for j in range(g)], axis=0
            )
            s = lax.dot_general(
                q, k_all[h], (((1,), (1,)), ((), ())), preferred_element_type=jnp.float32
            )
            s = s.reshape(g, rows, keys) * scale + bias[...][None]
            m = jnp.max(s, axis=-1, keepdims=True)
            p = jnp.exp2(s - m)
            total = jnp.sum(p, axis=-1, keepdims=True)
            o = jnp.dot(
                p.astype(jnp.bfloat16).reshape(g * rows, keys),
                v_all[h],
                preferred_element_type=jnp.float32,
            ).reshape(g, rows, HEAD)
            o = (o / total).astype(jnp.bfloat16)
            for j in range(g):
                o_buf[c, :, j * HEAD : (j + 1) * HEAD] = o[j]
            for d in range(n_tp):
                if h < local:
                    out_copy(c, lax.rem(tp + d + 1, n_tp)).start()
                else:
                    moved_out(c, d).start()
            return 0

        lax.fori_loop(0, per_kv, chunk, 0)
        if h == 0:
            for i in range(2):
                section_copy(i).wait_recv()
                for d in range(1, n_ctx):
                    kv_copy(i, local, d).start()
        if h == local - 1:
            section_copy(2).wait_recv()

    for i in range(3):
        section_copy(i).wait_send()
    for h in range(kv_heads):
        for i in range(2):
            for d in range(1, n_ctx):
                kv_copy(i, h, d).wait_send()

    def finish(c, _):
        for t in range(n_tp):
            out_copy(c, t).wait_send()
        for t in range(n_tp):
            there = out_hbm.at[0, :, lanes(t * q_cols + c * chunk_cols, chunk_cols)]
            pltpu.make_async_remote_copy(
                src_ref=there,
                dst_ref=there,
                send_sem=o_send.at[c, t],
                recv_sem=o_recv.at[c, t],
                device_id=(nxt, ctx, t),
                device_id_type=MESH,
            ).wait_recv()
        return 0

    def finish_moved(c, _):
        moved_out(c, 0).wait()
        for d in range(1, n_tp):
            moved_out(c, d).wait_send()
        for d in range(1, n_tp):
            t = lax.rem(tp + d, n_tp)
            there = out_hbm.at[0, :, lanes(t * q_cols + c * chunk_cols, chunk_cols)]
            pltpu.make_async_remote_copy(
                src_ref=there,
                dst_ref=there,
                send_sem=o_send.at[c, d],
                recv_sem=o_recv.at[c, t],
                device_id=(sec, ctx, t),
                device_id_type=MESH,
            ).wait_recv()
        return 0

    lax.fori_loop(local * per_kv, chunks, finish_moved, 0)
    lax.fori_loop(0, local * per_kv, finish, 0)


def shards(n_sec, n_ctx, n_tp, queries, keys, values, span_order):
    rows, q_cols, kv_cols = queries.shape[1], queries.shape[2], keys.shape[2]
    kv_heads = kv_cols // HEAD
    group = q_cols // kv_cols
    g = math.gcd(group, 4)
    chunks = q_cols // (g * HEAD)
    all_rows = rows * n_ctx
    dma = pltpu.SemaphoreType.DMA
    any_spec = pl.BlockSpec(memory_space=pl.ANY)
    return pl.pallas_call(
        functools.partial(kernel, n_sec, n_ctx, n_tp, g),
        out_shape=pltpu.VMEM((1, rows // n_tp, q_cols * n_tp), jnp.bfloat16),
        in_specs=[any_spec] * 4,
        out_specs=any_spec,
        scratch_shapes=[
            pltpu.VMEM((rows, q_cols), jnp.bfloat16),
            pltpu.VMEM((rows, group * HEAD), jnp.bfloat16),
            pltpu.VMEM((rows, kv_cols), jnp.bfloat16),
            pltpu.VMEM((rows, kv_cols), jnp.bfloat16),
            pltpu.VMEM((kv_heads, all_rows, HEAD), jnp.bfloat16),
            pltpu.VMEM((kv_heads, all_rows, HEAD), jnp.bfloat16),
            pltpu.VMEM((chunks, rows, g * HEAD), jnp.bfloat16),
            pltpu.VMEM((rows, all_rows), jnp.float32),
            pltpu.SMEM(span_order.shape, jnp.int32),
            dma((kv_heads,)),
            dma((2,)),
            dma,
            dma((kv_heads, 2, n_ctx)),
            dma((kv_heads, 2, n_ctx)),
            dma((3,)),
            dma((3,)),
            dma((chunks, n_tp)),
            dma((chunks, n_tp)),
        ],
        compiler_params=pltpu.CompilerParams(collective_id=0, has_side_effects=True),
    )(queries, keys, values, span_order)


def solution(mesh):
    sizes = [mesh.shape[axis] for axis in ("section", "ctx", "tp")]
    placed = P("section", "ctx", "tp")
    return jax.shard_map(
        functools.partial(shards, *sizes),
        mesh=mesh,
        in_specs=(placed, placed, placed, P()),
        out_specs=P("section", ("ctx", "tp"), None),
        check_vma=False,
    )
```

profile of v0, /device:TPU:0, one launch (start us, length us, event | category | flops | bytes accessed | tf_op | source)
XLA Modules:
  0.0 33.5 jit_solution(3772708470866558860)
XLA Ops:
  0.0 32.5 %shard_map.46 = bf16[1,64,8192]{2,1,0:T(8,128)(2,1)S(1)} custom-call(bf16[1,128,4096]{2,1,0:T(8,128)(2,1)} %q_hbm.1, bf16[1,128,512]{2,1,0:T(8,128)(2,1)} %k_hbm.1, bf16[1,128,512]{2,1,0:T(8,128)(2,1)} %v_hbm.1, s32[8]{0:T(128)} %order_hbm.1), custom_call_target="tpu_custom_call" | custom-call | tf_op jit(solution)/shard_map/pallas_call | solution.py:260
  32.5 1.0 %copy.6 = bf16[1,64,8192]{2,1,0:T(8,128)(2,1)} copy(bf16[1,64,8192]{2,1,0:T(8,128)(2,1)S(1)} %shard_map.46) | data formatting | bytes 2097152
where the time goes:
time: 33.6 us; the launch traced here: 33.5 us
  Pallas kernels  32.5 us (97%)
  local copies, waits for them, and re-layouts  0.97 us (3%)
    pallas_call x1, Pallas kernels, shards(): pl.pallas_call(functools.partial(kernel, n_sec, n_ctx, n_tp, g), out_shap...  32.5 us
    unnamed x1, local copies, waits for them, and re-layouts  0.97 us

commit v1 on v0

--- a/solution.py
+++ b/solution.py
@@ -189,14 +189,22 @@
             o = (o / total).astype(jnp.bfloat16)
             for j in range(g):
                 o_buf[c, :, j * HEAD : (j + 1) * HEAD] = o[j]
-            for d in range(n_tp):
-                if h < local:
-                    out_copy(c, lax.rem(tp + d + 1, n_tp)).start()
-                else:
+            if h < local:
+                out_copy(c, 0).start()
+
+                @pl.when(c > 0)
+                def _():
+                    for t in range(1, n_tp):
+                        out_copy(c - 1, t).start()
+            else:
+                for d in range(n_tp):
                     moved_out(c, d).start()
             return 0
 
         lax.fori_loop(0, per_kv, chunk, 0)
+        if h == local - 1:
+            for t in range(1, n_tp):
+                out_copy(local * per_kv - 1, t).start()
         if h == 0:
             for i in range(2):
                 section_copy(i).wait_recv()

time: 33.6 us -> 32.2 us (0.958)
  the two profiles are of different devices: /device:TPU:0 before, /device:TPU:5 now
where the time goes in v1:
time: 32.2 us; the launch traced here: 31.7 us
  Pallas kernels  30.8 us (96%)
  local copies, waits for them, and re-layouts  0.97 us (3%)
    pallas_call x1, Pallas kernels, shards(): pl.pallas_call(functools.partial(kernel, n_sec, n_ctx, n_tp, g), out_shap...  30.8 us
    unnamed x1, local copies, waits for them, and re-layouts  0.97 us

profile of v1, /device:TPU:5, one launch (start us, length us, event | category | flops | bytes accessed | tf_op | source)
XLA Modules:
  0.0 31.7 jit_solution(5673250206198498839)
XLA Ops:
  0.0 30.8 %shard_map.46 = bf16[1,64,8192]{2,1,0:T(8,128)(2,1)S(1)} custom-call(bf16[1,128,4096]{2,1,0:T(8,128)(2,1)} %q_hbm.1, bf16[1,128,512]{2,1,0:T(8,128)(2,1)} %k_hbm.1, bf16[1,128,512]{2,1,0:T(8,128)(2,1)} %v_hbm.1, s32[8]{0:T(128)} %order_hbm.1), custom_call_target="tpu_custom_call" | custom-call | tf_op jit(solution)/shard_map/pallas_call | solution.py:268
  30.8 1.0 %copy.6 = bf16[1,64,8192]{2,1,0:T(8,128)(2,1)} copy(bf16[1,64,8192]{2,1,0:T(8,128)(2,1)S(1)} %shard_map.46) | data formatting | bytes 2097152

commit v2 on v1

v2 whole, which is shorter than its diff:
```python
import functools
import math

import jax
import jax.numpy as jnp
from jax import lax
from jax.experimental import pallas as pl
from jax.experimental.pallas import tpu as pltpu
from jax.sharding import PartitionSpec as P

HEAD = 128
MESH = pl.DeviceIdType.MESH
NEG = -1e30
EARLY = 1


def lanes(start, size):
    return pl.ds(pl.multiple_of(start, HEAD), size)


def kernel(
    n_sec, n_ctx, n_tp, heads_per_chunk,
    q_hbm, k_hbm, v_hbm, order_hbm, out_hbm,
    q_buf, q_in, kv_own, kv_all, o_buf, bias, order,
    q_sem, own_sem, order_sem, kv_send, kv_recv, z_send, z_recv,
    o_send, o_recv, m_send, m_recv, m_own, ctx_in, tp_in, next_in,
):
    sec, ctx, tp = lax.axis_index("section"), lax.axis_index("ctx"), lax.axis_index("tp")
    rows, q_cols = q_hbm.shape[1], q_hbm.shape[2]
    kv_heads = k_hbm.shape[2] // HEAD
    group = q_cols // k_hbm.shape[2]
    g = heads_per_chunk
    chunk_cols = g * HEAD
    chunks = q_cols // chunk_cols
    per_kv = group // g
    out_rows = rows // n_tp
    keys = rows * n_ctx
    span = rows // 2
    local = kv_heads - 1
    group_cols = group * HEAD
    moved_cols = pl.ds(local * group_cols, group_cols)
    nxt, prv = lax.rem(sec + 1, n_sec), lax.rem(sec + n_sec - 1, n_sec)

    def there(s, c, t):
        return dict(device_id=(s, c, t), device_id_type=MESH)

    early = lax.rem(ctx, 2) == EARLY
    partner = ctx + 1 - 2 * lax.rem(ctx, 2)
    barrier = pltpu.get_barrier_semaphore()
    pl.semaphore_signal(barrier, inc=1, **there(prv, ctx, tp))
    for d in range(1, n_ctx):
        peer = lax.rem(ctx + d, n_ctx)

        @pl.when(lax.rem(peer, 2) != EARLY)
        def _():
            pl.semaphore_signal(barrier, inc=1, **there(sec, peer, tp))

    @pl.when(jnp.logical_not(early))
    def _():
        for d in range(1, n_tp):
            pl.semaphore_signal(barrier, inc=1, **there(sec, ctx, lax.rem(tp + d, n_tp)))

    def arrived(ref, sem):
        pltpu.make_async_copy(ref, ref, sem).wait()

    def left(ref, sem):
        pltpu.make_async_remote_copy(
            src_ref=ref, dst_ref=ref, send_sem=sem, recv_sem=sem, **there(nxt, ctx, tp)
        ).wait_send()

    for i, src in enumerate((k_hbm, v_hbm)):
        pltpu.make_async_copy(src.at[0], kv_own.at[i], own_sem).start()
    order_copy = pltpu.make_async_copy(order_hbm, order, order_sem)
    order_copy.start()
    for i, cols in enumerate((moved_cols, pl.ds(0, local * group_cols))):
        pltpu.make_async_copy(q_hbm.at[0, :, cols], q_buf.at[:, cols], q_sem.at[i]).start()

    arrived(kv_own, own_sem)

    def greet_tp():
        for d in range(1, n_tp):
            pl.semaphore_signal(next_in, inc=1, **there(sec, ctx, lax.rem(tp + d, n_tp)))

    pl.semaphore_wait(barrier, jnp.where(early, 1, n_ctx + n_tp - 1))

    @pl.when(jnp.logical_not(early))
    def _():
        pl.semaphore_signal(ctx_in, inc=1, **there(sec, partner, tp))
        greet_tp()

    others = pl.ds(0, keys - rows)
    mine = pl.ds(pl.multiple_of(ctx * rows, rows), rows)

    def kv_copy(i, h, d):
        dst = kv_all.at[h, i, mine, :]
        return pltpu.make_async_remote_copy(
            src_ref=kv_own.at[i, :, pl.ds(h * HEAD, HEAD)] if h < local else dst,
            dst_ref=dst,
            send_sem=kv_send,
            recv_sem=kv_recv.at[h],
            **there(sec, lax.rem(ctx + d, n_ctx), tp),
        )

    def section_copy(src, dst, recv_sem):
        return pltpu.make_async_remote_copy(
            src_ref=src, dst_ref=dst, send_sem=z_send, recv_sem=recv_sem, **there(nxt, ctx, tp)
        )

    for i in range(2):
        section_copy(
            kv_own.at[i, :, pl.ds(local * HEAD, HEAD)], kv_all.at[local, i, mine, :], z_recv.at[0]
        ).start()
    arrived(q_buf.at[:, moved_cols], q_sem.at[0])
    section_copy(q_buf.at[:, moved_cols], q_in, z_recv.at[1]).start()

    @pl.when(early)
    def _():
        pl.semaphore_wait(ctx_in, 1)

    for h in range(local):
        for i in range(2):
            for d in range(1, n_ctx):
                kv_copy(i, h, d).start()
    for h in range(local):
        for i in range(2):
            kv_all[h, i, mine, :] = kv_own[i, :, h * HEAD : (h + 1) * HEAD]

    order_copy.wait()
    row = lax.broadcasted_iota(jnp.int32, (rows, 1), 0)
    row_pos = jnp.where(row < span, order[2 * ctx] * span, order[2 * ctx + 1] * span - span) + row
    lane = lax.broadcasted_iota(jnp.int32, (1, keys), 1)
    key_pos = lane
    for j in range(keys // span):
        key_pos = jnp.where(
            (lane >= j * span) & (lane < (j + 1) * span), lane + (order[j] - j) * span, key_pos
        )
    bias[...] = jnp.where(key_pos <= row_pos, jnp.float32(0.0), jnp.float32(NEG))

    sent = local * per_kv
    late = 2
    scale = math.log2(math.e) / math.sqrt(HEAD)

    def out_copy(c, t):
        return pltpu.make_async_remote_copy(
            src_ref=o_buf.at[c, pl.ds(pl.multiple_of(t * out_rows, out_rows), out_rows), :],
            dst_ref=out_hbm.at[0, :, lanes(tp * q_cols + c * chunk_cols, chunk_cols)],
            send_sem=o_send,
            recv_sem=o_recv,
            **there(nxt, ctx, t),
        )

    def moved_out(c, d):
        t = lax.rem(tp + d, n_tp)
        src = o_buf.at[c, pl.ds(pl.multiple_of(t * out_rows, out_rows), out_rows), :]
        dst = out_hbm.at[0, :, lanes(tp * q_cols + c * chunk_cols, chunk_cols)]
        if d == 0:
            return pltpu.make_async_copy(src, dst, m_own)
        return pltpu.make_async_remote_copy(
            src_ref=src,
            dst_ref=dst,
            send_sem=m_send,
            recv_sem=m_recv,
            **there(sec, ctx, t),
        )

    for h in range(kv_heads):
        if h == 0:
            @pl.when(early)
            def _():
                pl.semaphore_wait(tp_in, 1)
                greet_tp()

            pl.semaphore_wait(next_in, n_tp - 1)

            @pl.when(jnp.logical_not(early))
            def _():
                pl.semaphore_signal(tp_in, inc=1, **there(sec, partner, tp))

            arrived(q_buf.at[:, pl.ds(0, local * group_cols)], q_sem.at[1])
        arrived(kv_all.at[h, :, others, :], kv_recv.at[h])

        def chunk(i, _, h=h):
            c = h * per_kv + i
            q_ref, first = (q_buf, c * g) if h < local else (q_in, i * g)
            q = jnp.concatenate(
                [q_ref[:, lanes((first + j) * HEAD, HEAD)] for j in range(g)], axis=0
            )
            s = lax.dot_general(
                q, kv_all[h, 0], (((1,), (1,)), ((), ())), preferred_element_type=jnp.float32
            )
            s = s.reshape(g, rows, keys) * scale + bias[...][None]
            m = jnp.max(s, axis=-1, keepdims=True)
            p = jnp.exp2(s - m)
            total = jnp.sum(p, axis=-1, keepdims=True)
            o = jnp.dot(
                p.astype(jnp.bfloat16).reshape(g * rows, keys),
                kv_all[h, 1],
                preferred_element_type=jnp.float32,
            ).reshape(g, rows, HEAD)
            o = (o / total).astype(jnp.bfloat16)
            for j in range(g):
                o_buf[c, :, j * HEAD : (j + 1) * HEAD] = o[j]
            if h < local:
                out_copy(c, 0).start()

                @pl.when(c >= late)
                def _():
                    for t in range(1, n_tp):
                        out_copy(c - late, t).start()
            else:
                for d in range(n_tp):
                    moved_out(c, d).start()
            return 0

        lax.fori_loop(0, per_kv, chunk, 0)
        if h == local - 1:
            for c in range(max(sent - late, 0), sent):
                for t in range(1, n_tp):
                    out_copy(c, t).start()
        if h == 0:
            arrived(kv_all.at[local, :, mine, :], z_recv.at[0])
            for i in range(2):
                for d in range(1, n_ctx):
                    kv_copy(i, local, d).start()
        if h == local - 1:
            arrived(q_in, z_recv.at[1])

    kept = chunks - sent
    left(q_buf.at[:, pl.ds(0, group_cols + 2 * HEAD)], z_send)
    left(kv_all.at[:, :, others, :], kv_send)
    arrived(out_hbm.at[0, :, pl.ds(0, kept * chunk_cols)], m_own)
    if n_tp > 1:
        moved = out_hbm.at[0, :, pl.ds(0, (n_tp - 1) * kept * chunk_cols)]
        left(moved, m_send)
        arrived(moved, m_recv)
    left(q_buf.at[:, pl.ds(0, sent * chunk_cols)], o_send)
    arrived(out_hbm.at[0, :, pl.ds(0, n_tp * sent * chunk_cols)], o_recv)


def shards(n_sec, n_ctx, n_tp, queries, keys, values, span_order):
    rows, q_cols, kv_cols = queries.shape[1], queries.shape[2], keys.shape[2]
    kv_heads = kv_cols // HEAD
    group = q_cols // kv_cols
    g = math.gcd(group, 4)
    chunks = q_cols // (g * HEAD)
    all_rows = rows * n_ctx
    dma = pltpu.SemaphoreType.DMA
    any_spec = pl.BlockSpec(memory_space=pl.ANY)
    return pl.pallas_call(
        functools.partial(kernel, n_sec, n_ctx, n_tp, g),
        out_shape=pltpu.VMEM((1, rows // n_tp, q_cols * n_tp), jnp.bfloat16),
        in_specs=[any_spec] * 4,
        out_specs=any_spec,
        scratch_shapes=[
            pltpu.VMEM((rows, q_cols), jnp.bfloat16),
            pltpu.VMEM((rows, group * HEAD), jnp.bfloat16),
            pltpu.VMEM((2, rows, kv_cols), jnp.bfloat16),
            pltpu.VMEM((kv_heads, 2, all_rows, HEAD), jnp.bfloat16),
            pltpu.VMEM((chunks, rows, g * HEAD), jnp.bfloat16),
            pltpu.VMEM((rows, all_rows), jnp.float32),
            pltpu.SMEM(span_order.shape, jnp.int32),
            dma((2,)),
            dma,
            dma,
            dma,
            dma((kv_heads,)),
            dma,
            dma((2,)),
            *[dma] * 5,
            *[pltpu.SemaphoreType.REGULAR] * 3,
        ],
        compiler_params=pltpu.CompilerParams(collective_id=0, has_side_effects=True),
    )(queries, keys, values, span_order)


def solution(mesh):
    sizes = [mesh.shape[axis] for axis in ("section", "ctx", "tp")]
    placed = P("section", "ctx", "tp")
    return jax.shard_map(
        functools.partial(shards, *sizes),
        mesh=mesh,
        in_specs=(placed, placed, placed, P()),
        out_specs=P("section", ("ctx", "tp"), None),
        check_vma=False,
    )
```

time: 32.2 us -> 30.8 us (0.957); the launches traced: 31.7 us -> 30.7 us
  Pallas kernels: 30.8 us -> 29.7 us
    pallas_call x1, Pallas kernels: 30.8 us -> 29.7 us  [shards(): pl.pallas_call(functools.partial(kernel, n_sec, n_ctx, n_tp, g), out_shap...]
where the time goes in v2:
time: 30.8 us; the launch traced here: 30.7 us
  Pallas kernels  29.7 us (96%)
  local copies, waits for them, and re-layouts  0.97 us (3%)
    pallas_call x1, Pallas kernels, shards(): pl.pallas_call(functools.partial(kernel, n_sec, n_ctx, n_tp, g), out_shap...  29.7 us
    unnamed x1, local copies, waits for them, and re-layouts  0.97 us

profile of v2, /device:TPU:5, one launch (start us, length us, event | category | flops | bytes accessed | tf_op | source)
XLA Modules:
  0.0 30.7 jit_solution(9387920046931268698)
XLA Ops:
  0.0 29.7 %shard_map.46 = bf16[1,64,8192]{2,1,0:T(8,128)(2,1)S(1)} custom-call(bf16[1,128,4096]{2,1,0:T(8,128)(2,1)} %q_hbm.1, bf16[1,128,512]{2,1,0:T(8,128)(2,1)} %k_hbm.1, bf16[1,128,512]{2,1,0:T(8,128)(2,1)} %v_hbm.1, s32[8]{0:T(128)} %order_hbm.1), custom_call_target="tpu_custom_call" | custom-call | tf_op jit(solution)/shard_map/pallas_call | solution.py:249
  29.7 1.0 %copy.6 = bf16[1,64,8192]{2,1,0:T(8,128)(2,1)} copy(bf16[1,64,8192]{2,1,0:T(8,128)(2,1)S(1)} %shard_map.46) | data formatting | bytes 2097152

commit v3 on v2

--- a/solution.py
+++ b/solution.py
@@ -21,9 +21,9 @@
 def kernel(
     n_sec, n_ctx, n_tp, heads_per_chunk,
     q_hbm, k_hbm, v_hbm, order_hbm, out_hbm,
-    q_buf, q_in, kv_own, kv_all, o_buf, bias, order,
+    q_buf, q_in, kv_own, kv_all, o_buf, relayed, bias, order,
     q_sem, own_sem, order_sem, kv_send, kv_recv, z_send, z_recv,
-    o_send, o_recv, m_send, m_recv, m_own, ctx_in, tp_in, next_in,
+    o_send, o_recv, m_send, m_recv, m_own, r_send, r_recv, ctx_in, tp_in, next_in,
 ):
     sec, ctx, tp = lax.axis_index("section"), lax.axis_index("ctx"), lax.axis_index("tp")
     rows, q_cols = q_hbm.shape[1], q_hbm.shape[2]
@@ -72,10 +72,8 @@
         pltpu.make_async_copy(src.at[0], kv_own.at[i], own_sem).start()
     order_copy = pltpu.make_async_copy(order_hbm, order, order_sem)
     order_copy.start()
-    for i, cols in enumerate((moved_cols, pl.ds(0, local * group_cols))):
-        pltpu.make_async_copy(q_hbm.at[0, :, cols], q_buf.at[:, cols], q_sem.at[i]).start()
-
-    arrived(kv_own, own_sem)
+    kept_cols = pl.ds(0, local * group_cols)
+    pltpu.make_async_copy(q_hbm.at[0, :, kept_cols], q_buf, q_sem).start()
 
     def greet_tp():
         for d in range(1, n_tp):
@@ -106,12 +104,12 @@
             src_ref=src, dst_ref=dst, send_sem=z_send, recv_sem=recv_sem, **there(nxt, ctx, tp)
         )
 
-    for i in range(2):
+    section_copy(q_hbm.at[0, :, moved_cols], q_in, z_recv.at[1]).start()
+    for i, src in enumerate((k_hbm, v_hbm)):
         section_copy(
-            kv_own.at[i, :, pl.ds(local * HEAD, HEAD)], kv_all.at[local, i, mine, :], z_recv.at[0]
+            src.at[0, :, pl.ds(local * HEAD, HEAD)], kv_all.at[local, i, mine, :], z_recv.at[0]
         ).start()
-    arrived(q_buf.at[:, moved_cols], q_sem.at[0])
-    section_copy(q_buf.at[:, moved_cols], q_in, z_recv.at[1]).start()
+    arrived(kv_own, own_sem)
 
     @pl.when(early)
     def _():
@@ -149,6 +147,57 @@
             **there(nxt, ctx, t),
         )
 
+    relay_rows = relayed.shape[0]
+    relays = n_tp > 1 and n_ctx % 4 == 0
+    gives = jnp.logical_and(lax.rem(ctx, 4) == 1, tp == 0)
+    takes = jnp.logical_and(lax.rem(ctx, 4) == 2, tp == 1)
+
+    def piece(c, first, size):
+        return o_buf.at[c, pl.ds(out_rows + first, size), :]
+
+    def give():
+        pltpu.make_async_remote_copy(
+            src_ref=piece(0, 0, relay_rows),
+            dst_ref=relayed,
+            send_sem=o_send,
+            recv_sem=r_recv,
+            **there(sec, lax.rem(ctx + 1, n_ctx), 1),
+        ).start()
+
+    def send_rest():
+        rest = pl.ds(relay_rows, out_rows - relay_rows)
+        pltpu.make_async_remote_copy(
+            src_ref=piece(0, relay_rows, out_rows - relay_rows),
+            dst_ref=out_hbm.at[0, rest, lanes(tp * q_cols, chunk_cols)],
+            send_sem=o_send,
+            recv_sem=o_recv,
+            **there(nxt, ctx, 1),
+        ).start()
+
+    def pass_on():
+        return pltpu.make_async_remote_copy(
+            src_ref=relayed,
+            dst_ref=out_hbm.at[0, pl.ds(0, relay_rows), pl.ds(0, chunk_cols)],
+            send_sem=r_send,
+            recv_sem=o_recv,
+            **there(nxt, lax.rem(ctx + n_ctx - 1, n_ctx), 1),
+        )
+
+    def send_late(c):
+        if not relays:
+            for t in range(1, n_tp):
+                out_copy(c, t).start()
+            return
+        given = jnp.logical_and(gives, c == 0)
+        pl.when(given)(send_rest)
+
+        @pl.when(jnp.logical_not(given))
+        def _():
+            out_copy(c, 1).start()
+
+        for t in range(2, n_tp):
+            out_copy(c, t).start()
+
     def moved_out(c, d):
         t = lax.rem(tp + d, n_tp)
         src = o_buf.at[c, pl.ds(pl.multiple_of(t * out_rows, out_rows), out_rows), :]
@@ -176,7 +225,7 @@
             def _():
                 pl.semaphore_signal(tp_in, inc=1, **there(sec, partner, tp))
 
-            arrived(q_buf.at[:, pl.ds(0, local * group_cols)], q_sem.at[1])
+            arrived(q_buf, q_sem)
         arrived(kv_all.at[h, :, others, :], kv_recv.at[h])
 
         def chunk(i, _, h=h):
@@ -201,12 +250,13 @@
             for j in range(g):
                 o_buf[c, :, j * HEAD : (j + 1) * HEAD] = o[j]
             if h < local:
+                if relays:
+                    pl.when(jnp.logical_and(gives, c == 0))(give)
                 out_copy(c, 0).start()
 
                 @pl.when(c >= late)
                 def _():
-                    for t in range(1, n_tp):
-                        out_copy(c - late, t).start()
+                    send_late(c - late)
             else:
                 for d in range(n_tp):
                     moved_out(c, d).start()
@@ -214,10 +264,15 @@
 
         lax.fori_loop(0, per_kv, chunk, 0)
         if h == local - 1:
+            if relays:
+                @pl.when(takes)
+                def _():
+                    arrived(relayed, r_recv)
+                    pass_on().start()
+
             for c in range(max(sent - late, 0), sent):
-                for t in range(1, n_tp):
-                    out_copy(c, t).start()
-        if h == 0:
+                send_late(c)
+        if h == min(1, local - 1):
             arrived(kv_all.at[local, :, mine, :], z_recv.at[0])
             for i in range(2):
                 for d in range(1, n_ctx):
@@ -226,14 +281,20 @@
             arrived(q_in, z_recv.at[1])
 
     kept = chunks - sent
-    left(q_buf.at[:, pl.ds(0, group_cols + 2 * HEAD)], z_send)
+    left(q_in, z_send)
+    left(kv_all.at[0, :, mine, :], z_send)
     left(kv_all.at[:, :, others, :], kv_send)
     arrived(out_hbm.at[0, :, pl.ds(0, kept * chunk_cols)], m_own)
     if n_tp > 1:
         moved = out_hbm.at[0, :, pl.ds(0, (n_tp - 1) * kept * chunk_cols)]
         left(moved, m_send)
         arrived(moved, m_recv)
-    left(q_buf.at[:, pl.ds(0, sent * chunk_cols)], o_send)
+    left(q_buf, o_send)
+    if relays:
+        @pl.when(takes)
+        def _():
+            pass_on().wait_send()
+
     arrived(out_hbm.at[0, :, pl.ds(0, n_tp * sent * chunk_cols)], o_recv)
 
 
@@ -252,21 +313,22 @@
         in_specs=[any_spec] * 4,
         out_specs=any_spec,
         scratch_shapes=[
-            pltpu.VMEM((rows, q_cols), jnp.bfloat16),
+            pltpu.VMEM((rows, q_cols - group * HEAD), jnp.bfloat16),
             pltpu.VMEM((rows, group * HEAD), jnp.bfloat16),
             pltpu.VMEM((2, rows, kv_cols), jnp.bfloat16),
             pltpu.VMEM((kv_heads, 2, all_rows, HEAD), jnp.bfloat16),
             pltpu.VMEM((chunks, rows, g * HEAD), jnp.bfloat16),
+            pltpu.VMEM((3 * rows // n_tp // 4, g * HEAD), jnp.bfloat16),
             pltpu.VMEM((rows, all_rows), jnp.float32),
             pltpu.SMEM(span_order.shape, jnp.int32),
+            dma,
+            dma,
+            dma,
+            dma,
+            dma((kv_heads,)),
+            dma,
             dma((2,)),
-            dma,
-            dma,
-            dma,
-            dma((kv_heads,)),
-            dma,
-            dma((2,)),
-            *[dma] * 5,
+            *[dma] * 7,
             *[pltpu.SemaphoreType.REGULAR] * 3,
         ],
         compiler_params=pltpu.CompilerParams(collective_id=0, has_side_effects=True),

time: 30.8 us -> 30.4 us (0.987)
  Pallas kernels: 29.7 us -> 29.3 us
    pallas_call x1, Pallas kernels: 29.7 us -> 29.3 us  [shards(): pl.pallas_call(functools.partial(kernel, n_sec, n_ctx, n_tp, g), out_shap...]
where the time goes in v3:
time: 30.4 us; the launch traced here: 30.3 us
  Pallas kernels  29.3 us (96%)
  local copies, waits for them, and re-layouts  0.97 us (3%)
    pallas_call x1, Pallas kernels, shards(): pl.pallas_call(functools.partial(kernel, n_sec, n_ctx, n_tp, g), out_shap...  29.3 us
    unnamed x1, local copies, waits for them, and re-layouts  0.97 us

profile of v3, /device:TPU:5, one launch (start us, length us, event | category | flops | bytes accessed | tf_op | source)
XLA Modules:
  0.0 30.3 jit_solution(12697985288816471295)
XLA Ops:
  0.0 29.3 %shard_map.46 = bf16[1,64,8192]{2,1,0:T(8,128)(2,1)S(1)} custom-call(bf16[1,128,4096]{2,1,0:T(8,128)(2,1)} %q_hbm.1, bf16[1,128,512]{2,1,0:T(8,128)(2,1)} %k_hbm.1, bf16[1,128,512]{2,1,0:T(8,128)(2,1)} %v_hbm.1, s32[8]{0:T(128)} %order_hbm.1), custom_call_target="tpu_custom_call" | custom-call | tf_op jit(solution)/shard_map/pallas_call | solution.py:310
  29.3 1.0 %copy.6 = bf16[1,64,8192]{2,1,0:T(8,128)(2,1)} copy(bf16[1,64,8192]{2,1,0:T(8,128)(2,1)S(1)} %shard_map.46) | data formatting | bytes 2097152

commit v4 on v3

--- a/solution.py
+++ b/solution.py
@@ -68,12 +68,16 @@
             src_ref=ref, dst_ref=ref, send_sem=sem, recv_sem=sem, **there(nxt, ctx, tp)
         ).wait_send()
 
-    for i, src in enumerate((k_hbm, v_hbm)):
-        pltpu.make_async_copy(src.at[0], kv_own.at[i], own_sem).start()
+    kept_cols = pl.ds(0, local * group_cols)
     order_copy = pltpu.make_async_copy(order_hbm, order, order_sem)
-    order_copy.start()
-    kept_cols = pl.ds(0, local * group_cols)
-    pltpu.make_async_copy(q_hbm.at[0, :, kept_cols], q_buf, q_sem).start()
+
+    def load():
+        for i, src in enumerate((k_hbm, v_hbm)):
+            pltpu.make_async_copy(src.at[0], kv_own.at[i], own_sem).start()
+        order_copy.start()
+        pltpu.make_async_copy(q_hbm.at[0, :, kept_cols], q_buf, q_sem).start()
+
+    pl.when(jnp.logical_not(early))(load)
 
     def greet_tp():
         for d in range(1, n_tp):
@@ -109,6 +113,7 @@
         section_copy(
             src.at[0, :, pl.ds(local * HEAD, HEAD)], kv_all.at[local, i, mine, :], z_recv.at[0]
         ).start()
+    pl.when(early)(load)
     arrived(kv_own, own_sem)
 
     @pl.when(early)
@@ -135,7 +140,7 @@
     bias[...] = jnp.where(key_pos <= row_pos, jnp.float32(0.0), jnp.float32(NEG))
 
     sent = local * per_kv
-    late = 2
+    late = 4
     scale = math.log2(math.e) / math.sqrt(HEAD)
 
     def out_copy(c, t):
@@ -147,55 +152,36 @@
             **there(nxt, ctx, t),
         )
 
-    relay_rows = relayed.shape[0]
+    n_relay = relayed.shape[0]
     relays = n_tp > 1 and n_ctx % 4 == 0
     gives = jnp.logical_and(lax.rem(ctx, 4) == 1, tp == 0)
     takes = jnp.logical_and(lax.rem(ctx, 4) == 2, tp == 1)
 
-    def piece(c, first, size):
-        return o_buf.at[c, pl.ds(out_rows + first, size), :]
-
-    def give():
+    def give(c):
         pltpu.make_async_remote_copy(
-            src_ref=piece(0, 0, relay_rows),
-            dst_ref=relayed,
+            src_ref=o_buf.at[c, pl.ds(out_rows, out_rows), :],
+            dst_ref=relayed.at[c],
             send_sem=o_send,
             recv_sem=r_recv,
             **there(sec, lax.rem(ctx + 1, n_ctx), 1),
         ).start()
 
-    def send_rest():
-        rest = pl.ds(relay_rows, out_rows - relay_rows)
-        pltpu.make_async_remote_copy(
-            src_ref=piece(0, relay_rows, out_rows - relay_rows),
-            dst_ref=out_hbm.at[0, rest, lanes(tp * q_cols, chunk_cols)],
-            send_sem=o_send,
-            recv_sem=o_recv,
-            **there(nxt, ctx, 1),
-        ).start()
-
-    def pass_on():
-        return pltpu.make_async_remote_copy(
-            src_ref=relayed,
-            dst_ref=out_hbm.at[0, pl.ds(0, relay_rows), pl.ds(0, chunk_cols)],
+    def pass_on(c):
+        return pltpu.make_async_remote_copy(
+            src_ref=relayed.at[c],
+            dst_ref=out_hbm.at[0, :, pl.ds(c * chunk_cols, chunk_cols)],
             send_sem=r_send,
             recv_sem=o_recv,
             **there(nxt, lax.rem(ctx + n_ctx - 1, n_ctx), 1),
         )
 
     def send_late(c):
-        if not relays:
-            for t in range(1, n_tp):
-                out_copy(c, t).start()
-            return
-        given = jnp.logical_and(gives, c == 0)
-        pl.when(given)(send_rest)
-
-        @pl.when(jnp.logical_not(given))
-        def _():
-            out_copy(c, 1).start()
-
-        for t in range(2, n_tp):
+        if relays:
+            @pl.when(jnp.logical_not(jnp.logical_and(gives, c < n_relay)))
+            def _():
+                out_copy(c, 1).start()
+
+        for t in range(2 if relays else 1, n_tp):
             out_copy(c, t).start()
 
     def moved_out(c, d):
@@ -251,7 +237,10 @@
                 o_buf[c, :, j * HEAD : (j + 1) * HEAD] = o[j]
             if h < local:
                 if relays:
-                    pl.when(jnp.logical_and(gives, c == 0))(give)
+                    @pl.when(jnp.logical_and(gives, c < n_relay))
+                    def _():
+                        give(c)
+
                 out_copy(c, 0).start()
 
                 @pl.when(c >= late)
@@ -268,7 +257,8 @@
                 @pl.when(takes)
                 def _():
                     arrived(relayed, r_recv)
-                    pass_on().start()
+                    for c in range(n_relay):
+                        pass_on(c).start()
 
             for c in range(max(sent - late, 0), sent):
                 send_late(c)
@@ -293,7 +283,7 @@
     if relays:
         @pl.when(takes)
         def _():
-            pass_on().wait_send()
+            left(relayed, r_send)
 
     arrived(out_hbm.at[0, :, pl.ds(0, n_tp * sent * chunk_cols)], o_recv)
 
@@ -302,7 +292,8 @@
     rows, q_cols, kv_cols = queries.shape[1], queries.shape[2], keys.shape[2]
     kv_heads = kv_cols // HEAD
     group = q_cols // kv_cols
-    g = math.gcd(group, 4)
+    g = math.gcd(group, 2)
+    relay = 1
     chunks = q_cols // (g * HEAD)
     all_rows = rows * n_ctx
     dma = pltpu.SemaphoreType.DMA
@@ -318,7 +309,7 @@
             pltpu.VMEM((2, rows, kv_cols), jnp.bfloat16),
             pltpu.VMEM((kv_heads, 2, all_rows, HEAD), jnp.bfloat16),
             pltpu.VMEM((chunks, rows, g * HEAD), jnp.bfloat16),
-            pltpu.VMEM((3 * rows // n_tp // 4, g * HEAD), jnp.bfloat16),
+            pltpu.VMEM((relay, rows // n_tp, g * HEAD), jnp.bfloat16),
             pltpu.VMEM((rows, all_rows), jnp.float32),
             pltpu.SMEM(span_order.shape, jnp.int32),
             dma,

time: 30.4 us -> 30.1 us (level)
  no operation moved by 1% of the time
where the time goes in v4:
time: 30.1 us; the launch traced here: 30 us
  Pallas kernels  29 us (96%)
  local copies, waits for them, and re-layouts  0.97 us (3%)
    pallas_call x1, Pallas kernels, shards(): pl.pallas_call(functools.partial(kernel, n_sec, n_ctx, n_tp, g), out_shap...  29 us
    unnamed x1, local copies, waits for them, and re-layouts  0.97 us

profile of v4, /device:TPU:5, one launch (start us, length us, event | category | flops | bytes accessed | tf_op | source)
XLA Modules:
  0.0 30.0 jit_solution(15985036202876730430)
XLA Ops:
  0.0 29.0 %shard_map.46 = bf16[1,64,8192]{2,1,0:T(8,128)(2,1)S(1)} custom-call(bf16[1,128,4096]{2,1,0:T(8,128)(2,1)} %q_hbm.1, bf16[1,128,512]{2,1,0:T(8,128)(2,1)} %k_hbm.1, bf16[1,128,512]{2,1,0:T(8,128)(2,1)} %v_hbm.1, s32[8]{0:T(128)} %order_hbm.1), custom_call_target="tpu_custom_call" | custom-call | tf_op jit(solution)/shard_map/pallas_call | solution.py:301
  29.0 1.0 %copy.6 = bf16[1,64,8192]{2,1,0:T(8,128)(2,1)} copy(bf16[1,64,8192]{2,1,0:T(8,128)(2,1)S(1)} %shard_map.46) | data formatting | bytes 2097152

commit v5 on v4

--- a/solution.py
+++ b/solution.py
@@ -22,8 +22,7 @@
     n_sec, n_ctx, n_tp, heads_per_chunk,
     q_hbm, k_hbm, v_hbm, order_hbm, out_hbm,
     q_buf, q_in, kv_own, kv_all, o_buf, relayed, bias, order,
-    q_sem, own_sem, order_sem, kv_send, kv_recv, z_send, z_recv,
-    o_send, o_recv, m_send, m_recv, m_own, r_send, r_recv, ctx_in, tp_in, next_in,
+    q_sem, own_sem, order_sem, sends, kv_recv, z_recv, o_recv, r_recv, pair_in, next_in,
 ):
     sec, ctx, tp = lax.axis_index("section"), lax.axis_index("ctx"), lax.axis_index("tp")
     rows, q_cols = q_hbm.shape[1], q_hbm.shape[2]
@@ -87,7 +86,7 @@
 
     @pl.when(jnp.logical_not(early))
     def _():
-        pl.semaphore_signal(ctx_in, inc=1, **there(sec, partner, tp))
+        pl.semaphore_signal(pair_in, inc=1, **there(sec, partner, tp))
         greet_tp()
 
     others = pl.ds(0, keys - rows)
@@ -98,14 +97,14 @@
         return pltpu.make_async_remote_copy(
             src_ref=kv_own.at[i, :, pl.ds(h * HEAD, HEAD)] if h < local else dst,
             dst_ref=dst,
-            send_sem=kv_send,
+            send_sem=sends,
             recv_sem=kv_recv.at[h],
             **there(sec, lax.rem(ctx + d, n_ctx), tp),
         )
 
     def section_copy(src, dst, recv_sem):
         return pltpu.make_async_remote_copy(
-            src_ref=src, dst_ref=dst, send_sem=z_send, recv_sem=recv_sem, **there(nxt, ctx, tp)
+            src_ref=src, dst_ref=dst, send_sem=sends, recv_sem=recv_sem, **there(nxt, ctx, tp)
         )
 
     section_copy(q_hbm.at[0, :, moved_cols], q_in, z_recv.at[1]).start()
@@ -118,7 +117,7 @@
 
     @pl.when(early)
     def _():
-        pl.semaphore_wait(ctx_in, 1)
+        pl.semaphore_wait(pair_in, 1)
 
     for h in range(local):
         for i in range(2):
@@ -147,7 +146,7 @@
         return pltpu.make_async_remote_copy(
             src_ref=o_buf.at[c, pl.ds(pl.multiple_of(t * out_rows, out_rows), out_rows), :],
             dst_ref=out_hbm.at[0, :, lanes(tp * q_cols + c * chunk_cols, chunk_cols)],
-            send_sem=o_send,
+            send_sem=sends,
             recv_sem=o_recv,
             **there(nxt, ctx, t),
         )
@@ -161,7 +160,7 @@
         pltpu.make_async_remote_copy(
             src_ref=o_buf.at[c, pl.ds(out_rows, out_rows), :],
             dst_ref=relayed.at[c],
-            send_sem=o_send,
+            send_sem=sends,
             recv_sem=r_recv,
             **there(sec, lax.rem(ctx + 1, n_ctx), 1),
         ).start()
@@ -170,7 +169,7 @@
         return pltpu.make_async_remote_copy(
             src_ref=relayed.at[c],
             dst_ref=out_hbm.at[0, :, pl.ds(c * chunk_cols, chunk_cols)],
-            send_sem=r_send,
+            send_sem=sends,
             recv_sem=o_recv,
             **there(nxt, lax.rem(ctx + n_ctx - 1, n_ctx), 1),
         )
@@ -189,12 +188,12 @@
         src = o_buf.at[c, pl.ds(pl.multiple_of(t * out_rows, out_rows), out_rows), :]
         dst = out_hbm.at[0, :, lanes(tp * q_cols + c * chunk_cols, chunk_cols)]
         if d == 0:
-            return pltpu.make_async_copy(src, dst, m_own)
+            return pltpu.make_async_copy(src, dst, o_recv)
         return pltpu.make_async_remote_copy(
             src_ref=src,
             dst_ref=dst,
-            send_sem=m_send,
-            recv_sem=m_recv,
+            send_sem=sends,
+            recv_sem=o_recv,
             **there(sec, ctx, t),
         )
 
@@ -202,14 +201,14 @@
         if h == 0:
             @pl.when(early)
             def _():
-                pl.semaphore_wait(tp_in, 1)
+                pl.semaphore_wait(pair_in, 1)
                 greet_tp()
 
             pl.semaphore_wait(next_in, n_tp - 1)
 
             @pl.when(jnp.logical_not(early))
             def _():
-                pl.semaphore_signal(tp_in, inc=1, **there(sec, partner, tp))
+                pl.semaphore_signal(pair_in, inc=1, **there(sec, partner, tp))
 
             arrived(q_buf, q_sem)
         arrived(kv_all.at[h, :, others, :], kv_recv.at[h])
@@ -271,21 +270,18 @@
             arrived(q_in, z_recv.at[1])
 
     kept = chunks - sent
-    left(q_in, z_send)
-    left(kv_all.at[0, :, mine, :], z_send)
-    left(kv_all.at[:, :, others, :], kv_send)
-    arrived(out_hbm.at[0, :, pl.ds(0, kept * chunk_cols)], m_own)
+    left(q_in, sends)
+    left(kv_all.at[0, :, mine, :], sends)
+    left(kv_all.at[:, :, others, :], sends)
     if n_tp > 1:
-        moved = out_hbm.at[0, :, pl.ds(0, (n_tp - 1) * kept * chunk_cols)]
-        left(moved, m_send)
-        arrived(moved, m_recv)
-    left(q_buf, o_send)
+        left(out_hbm.at[0, :, pl.ds(0, (n_tp - 1) * kept * chunk_cols)], sends)
+    left(q_buf, sends)
     if relays:
         @pl.when(takes)
         def _():
-            left(relayed, r_send)
-
-    arrived(out_hbm.at[0, :, pl.ds(0, n_tp * sent * chunk_cols)], o_recv)
+            left(relayed, sends)
+
+    arrived(out_hbm.at[0], o_recv)
 
 
 def shards(n_sec, n_ctx, n_tp, queries, keys, values, span_order):
@@ -312,15 +308,11 @@
             pltpu.VMEM((relay, rows // n_tp, g * HEAD), jnp.bfloat16),
             pltpu.VMEM((rows, all_rows), jnp.float32),
             pltpu.SMEM(span_order.shape, jnp.int32),
-            dma,
-            dma,
-            dma,
-            dma,
+            *[dma] * 4,
             dma((kv_heads,)),
-            dma,
             dma((2,)),
-            *[dma] * 7,
-            *[pltpu.SemaphoreType.REGULAR] * 3,
+            *[dma] * 2,
+            *[pltpu.SemaphoreType.REGULAR] * 2,
         ],
         compiler_params=pltpu.CompilerParams(collective_id=0, has_side_effects=True),
     )(queries, keys, values, span_order)

time: 30.1 us -> 30.1 us (level)
  no operation moved by 1% of the time
where the time goes in v5:
time: 30.1 us; the launch traced here: 29.9 us
  Pallas kernels  29 us (96%)
  local copies, waits for them, and re-layouts  0.97 us (3%)
    pallas_call x1, Pallas kernels, shards(): pl.pallas_call(functools.partial(kernel, n_sec, n_ctx, n_tp, g), out_shap...  29 us
    unnamed x1, local copies, waits for them, and re-layouts  0.97 us

profile of v5, /device:TPU:5, one launch (start us, length us, event | category | flops | bytes accessed | tf_op | source)
XLA Modules:
  0.0 29.9 jit_solution(6291970510264999695)
XLA Ops:
  0.0 29.0 %shard_map.46 = bf16[1,64,8192]{2,1,0:T(8,128)(2,1)S(1)} custom-call(bf16[1,128,4096]{2,1,0:T(8,128)(2,1)} %q_hbm.1, bf16[1,128,512]{2,1,0:T(8,128)(2,1)} %k_hbm.1, bf16[1,128,512]{2,1,0:T(8,128)(2,1)} %v_hbm.1, s32[8]{0:T(128)} %order_hbm.1), custom_call_target="tpu_custom_call" | custom-call | tf_op jit(solution)/shard_map/pallas_call | solution.py:297
  29.0 1.0 %copy.6 = bf16[1,64,8192]{2,1,0:T(8,128)(2,1)} copy(bf16[1,64,8192]{2,1,0:T(8,128)(2,1)S(1)} %shard_map.46) | data formatting | bytes 2097152

commit v6 on v5

--- a/solution.py
+++ b/solution.py
@@ -139,7 +139,7 @@
     bias[...] = jnp.where(key_pos <= row_pos, jnp.float32(0.0), jnp.float32(NEG))
 
     sent = local * per_kv
-    late = 4
+    late = 3
     scale = math.log2(math.e) / math.sqrt(HEAD)
 
     def out_copy(c, t):

time: 30.1 us -> 30.1 us (level)
  no operation moved by 1% of the time
where the time goes in v6:
time: 30.1 us; the launch traced here: 29.9 us
  Pallas kernels  29 us (96%)
  local copies, waits for them, and re-layouts  0.97 us (3%)
    pallas_call x1, Pallas kernels, shards(): pl.pallas_call(functools.partial(kernel, n_sec, n_ctx, n_tp, g), out_shap...  29 us
    unnamed x1, local copies, waits for them, and re-layouts  0.97 us

profile of v6, /device:TPU:5, one launch (start us, length us, event | category | flops | bytes accessed | tf_op | source)
XLA Modules:
  0.0 29.9 jit_solution(1407928823568232114)
XLA Ops:
  0.0 29.0 %shard_map.46 = bf16[1,64,8192]{2,1,0:T(8,128)(2,1)S(1)} custom-call(bf16[1,128,4096]{2,1,0:T(8,128)(2,1)} %q_hbm.1, bf16[1,128,512]{2,1,0:T(8,128)(2,1)} %k_hbm.1, bf16[1,128,512]{2,1,0:T(8,128)(2,1)} %v_hbm.1, s32[8]{0:T(128)} %order_hbm.1), custom_call_target="tpu_custom_call" | custom-call | tf_op jit(solution)/shard_map/pallas_call | solution.py:297
  29.0 1.0 %copy.6 = bf16[1,64,8192]{2,1,0:T(8,128)(2,1)} copy(bf16[1,64,8192]{2,1,0:T(8,128)(2,1)S(1)} %shard_map.46) | data formatting | bytes 2097152
